TPU v7x, 32 devices: a whole 2x2x4 slice. The times are simulated.
32 devices in a mesh: stream: 8 (over z, x), span: 4 (over y, core).
Axes of the slice: x: 2, y: 2, z: 4, core: 2. Of those that a mesh axis runs over, the one named last changes fastest.
Arguments:
- state: float32 [320, 8, 625], P('stream', 'span'), may hold values from -0.25 to 2.5, as said below
- direction: float32 [320, 8, 625], P('stream', 'span'), may hold values from -6 to 6
- metric: float32 [320, 8, 3], P('stream', 'span'), may hold values from 1 to 4
- face_source: int32 [320, 4], P('stream'), may hold values from -1 to 225, as said below
- send_rows: int32 [8, 2, 33], P('stream'), may hold values from 0 to 159, as said below
Outputs:
- residual: float32 [320, 8, 625], P('stream', 'span')
- basis_next: float32 [320, 8, 625], P('stream', 'span')
- krylov: float32 [3], replicated
Inputs may be any that keep to these rules, and one draw needn't show every extreme that they name: `state`: conserved variables from density 0.75 to 1.25, flow-wise velocity 0.1 to 0.5, other velocities -0.2 to 0.2, pressure 0.5 to 0.9, so pressure and temperature are positive. `face_source`: the plane is a grid of columns of 32 cells, numbered column by column, partition d owning cells d * 40 to (d + 1) * 40 - 1 in a random local order; flow-wise faces wrap around. Every face neighbour lies in the same or an adjacent partition; -1 stands exactly on the lower face of the lowest and the upper face of the highest row; indices into received blocks point at used slots. `send_rows`: at most 33 faces per neighbouring pair, and some pair uses all 33; slots beyond a pair's count hold 0; the order of slots is the order in which the receiver's face_source refers to them.
All inputs are finite; a program needn't handle non-finite values.
Results may differ from a plain program's by a relative error of at most 0.0003.
Values sent between devices are 32-bit elements.
A program may use at most 128 MiB of HBM per device.

v0:
```python
import functools
import math

import jax
import jax.numpy as jnp
import numpy as np
from jax import lax
from jax.experimental import pallas as pl
from jax.experimental.pallas import tpu as pltpu
from jax.sharding import PartitionSpec as P

GAMMA = 1.4
VISC = 0.01
COND = VISC * GAMMA / ((GAMMA - 1.0) * 0.72)
LIFT = 10.0
MESH = pl.DeviceIdType.MESH
F32, BF16 = jnp.float32, jnp.bfloat16


def diff_table():
    spread = math.sqrt(3.0 / 7.0)
    points = np.array([-1.0, -spread, 0.0, spread, 1.0])
    weights = np.array(
        [np.prod([points[i] - points[j] for j in range(5) if j != i]) for i in range(5)]
    )
    matrix = np.zeros((5, 5))
    for i in range(5):
        for j in range(5):
            if i != j:
                matrix[i, j] = weights[i] / (weights[j] * (points[i] - points[j]))
        matrix[i, i] = np.sum([1.0 / (points[i] - points[j]) for j in range(5) if j != i])
    return matrix


def operators(layers):
    table = diff_table()
    eye = np.eye(5)
    kron = [
        np.einsum("ai,bj,ck->ijkabc", *[table if m == a else eye for m in range(3)]).reshape(125, 125)
        for a in range(3)
    ]
    node = np.arange(125).reshape(5, 5, 5)
    vw, fw, half = 128 * layers, 64 * layers, 32 * layers
    deriv = np.zeros((3, vw, vw), np.float32)
    pick = np.zeros((3, vw, fw), np.float32)
    for a in range(3):
        for l in range(layers):
            b = 128 * l
            deriv[a, b : b + 125, b : b + 125] = kron[a]
            for side in range(2):
                face = np.take(node, 4 * side, axis=a).reshape(-1)
                for m, at in enumerate(face):
                    pick[a, b + at, side * half + 32 * l + m] = 1.0
    high = deriv.astype(jnp.bfloat16)
    low = (deriv - high.astype(np.float32)).astype(jnp.bfloat16)
    lift = np.swapaxes(pick, 1, 2)
    return high, low, pick.astype(jnp.bfloat16), lift.astype(jnp.bfloat16)


def pieces(x, n):
    out = []
    for i in range(n):
        p = x.astype(BF16)
        out.append(p)
        if i + 1 < n:
            x = x - p.astype(F32)
    return out


def dot(a, b):
    return jnp.dot(a, b, preferred_element_type=F32)


def left(x, w, n):
    return sum(dot(p, w) for p in pieces(x, n)[::-1])


def right(w, x, n):
    return sum(dot(w, p) for p in pieces(x, n)[::-1])


def derive(x, high, low):
    a, b = pieces(x, 2)
    return dot(a, low) + dot(b, high) + dot(a, high)


def fields_of(u):
    inv = 1.0 / u[0]
    vel = [u[1] * inv, u[2] * inv, u[3] * inv]
    kinetic = 0.5 * (u[1] * vel[0] + u[2] * vel[1] + u[3] * vel[2])
    pressure = (GAMMA - 1.0) * (u[4] - kinetic)
    return vel, pressure, pressure * inv


def inviscid(u, a):
    vel, pressure, _ = fields_of(u)
    out = [u[1 + a]]
    for m in range(3):
        term = u[1 + m] * vel[a]
        out.append(term + pressure if m == a else term)
    out.append((u[4] + pressure) * vel[a])
    return out


def viscous(vel, q, a, divergence):
    stress = []
    for m in range(3):
        term = q[a][m] + q[m][a]
        if m == a:
            term = term - 2.0 / 3.0 * divergence
        stress.append(VISC * term)
    energy = stress[0] * vel[0] + stress[1] * vel[1] + stress[2] * vel[2] + COND * q[a][3]
    return stress + [energy]


def viscous_all(u, q):
    inv = 1.0 / u[0]
    vel = [u[1] * inv, u[2] * inv, u[3] * inv]
    divergence = q[0][0] + q[1][1] + q[2][2]
    return [viscous(vel, q, a, divergence) for a in range(3)]


def gradient_fields(u):
    vel, _, temper = fields_of(u)
    return vel + [temper]


def jump_fields(inner, outer):
    return [o - i for o, i in zip(gradient_fields(outer), gradient_fields(inner))]


def surface(inner, outer, sign, a):
    vi, pi, ti = fields_of(inner)
    vo, po, to = fields_of(outer)
    square = sum(v * v for v in vi) + GAMMA * ti + sum(v * v for v in vo) + GAMMA * to
    speed = jnp.sqrt(0.5 * square)
    fi, fo = inviscid(inner, a), inviscid(outer, a)
    return [
        (0.5 * LIFT) * (sign * (fo[m] - fi[m]) - speed * (outer[m] - inner[m])) for m in range(5)
    ]


def kernel(
    ns, np_, total_count,
    x_ref, d_ref, metric_ref, fs_ref, sr_ref, keyrow_ref, dh_ref, dl_ref, pick_ref, lift_ref,
    res_ref, basis_ref, kry_ref,
    u, uf, of, w, jf, q, v, vf, ov, g, s, r, mv, mf,
    sb1, rb1, zs1, zr1, sb2, rb2, zs2, zr2, st, sta, stb,
    xsend, xrecv, asend, arecv, bsend, brecv,
):
    C, L = x_ref.shape[0], x_ref.shape[1]
    VW, FW, half = 128 * L, 64 * L, 32 * L
    SLOTS = sr_ref.shape[2]
    SP = sb1.shape[1]
    OWN = 4 * C
    ms, mp = lax.axis_index("stream"), lax.axis_index("span")
    lower, upper = lax.rem(ms + ns - 1, ns), lax.rem(ms + 1, ns)
    below, above = lax.rem(mp + np_ - 1, np_), lax.rem(mp + 1, np_)

    barrier = pltpu.get_barrier_semaphore()
    for k in range(1, ns):
        pl.semaphore_signal(
            barrier, inc=1, device_id=(lax.rem(ms + k, ns), mp), device_id_type=MESH
        )
    for k in range(1, np_):
        pl.semaphore_signal(
            barrier, inc=1, device_id=(ms, lax.rem(mp + k, np_)), device_id_type=MESH
        )

    fl = lax.broadcasted_iota(jnp.int32, (1, FW), 1)
    vl = lax.broadcasted_iota(jnp.int32, (1, VW), 1)
    first = fl < half
    sign = jnp.where(first, -1.0, 1.0)
    flayer = lax.rem(fl, half) // 32
    fpad = jnp.where(lax.rem(fl, 32) >= 25, 1.0, 0.0)

    for pt, ref in enumerate((x_ref, d_ref)):
        for l in range(L):
            for m in range(5):
                pad = 1.0 if pt == 0 and m % 4 == 0 else 0.0
                u[pt, m, :, 128 * l + 120 : 128 * (l + 1)] = jnp.full((C, 8), pad, F32)
                u[pt, m, :, 128 * l : 128 * l + 125] = ref[:, l, 125 * m : 125 * (m + 1)]
    for a in range(3):
        wide = jnp.zeros((C, VW), F32)
        face = jnp.zeros((C, FW), F32)
        for l in range(L):
            value = metric_ref[:, l, a : a + 1]
            wide = jnp.where(vl // 128 == l, value, wide)
            face = jnp.where(flayer == l, value, face)
        mv[a] = wide
        mf[a] = face

    keyrow = keyrow_ref[...]
    onehot = jnp.concatenate(
        [
            jnp.where(fs_ref[:, 2 * a + side : 2 * a + side + 1] == keyrow, 1.0, 0.0)
            for side in range(2)
            for a in range(2)
        ],
        axis=0,
    ).astype(BF16)
    hot_own, hot_recv = onehot[:, :OWN], onehot[:, OWN : OWN + 2 * SP]
    ri = lax.broadcasted_iota(jnp.int32, (SP, SLOTS), 0)
    li = lax.broadcasted_iota(jnp.int32, (SP, SLOTS), 1)
    send_hot = []
    for side in range(2):
        row = sr_ref[0, side : side + 1, :].astype(F32)
        column = jnp.sum(jnp.where(ri == li, row, 0.0), axis=1, keepdims=True)
        send_hot.append(jnp.where(column == keyrow[:, :OWN].astype(F32), 1.0, 0.0))
    send_hot = jnp.concatenate(send_hot, axis=0).astype(BF16)

    def swap(a, b):
        return (
            jnp.where(first, a, pltpu.roll(b, half, 1)),
            jnp.where(first, pltpu.roll(a, half, 1), b),
        )

    def exchange(faces, members, sb, rb, zs, zr, base):
        blocks = [[swap(faces(0, m, a), faces(1, m, a)) for m in range(members)] for a in range(3)]
        table = jnp.concatenate(
            [
                jnp.concatenate([blocks[a][m][side] for m in range(members)], axis=1)
                for side in range(2)
                for a in range(2)
            ],
            axis=0,
        )
        for side in range(2):
            for m in range(members):
                zs[side, :, FW * m : FW * (m + 1)] = blocks[2][m][side]
        zs_copies = [
            (zs.at[0], zr.at[1], (ms, below)),
            (zs.at[1], zr.at[0], (ms, above)),
        ]
        copies = []
        for i, (src, dst, to) in enumerate(zs_copies):
            copies.append(
                pltpu.make_async_remote_copy(
                    src_ref=src, dst_ref=dst, send_sem=xsend.at[base + i],
                    recv_sem=xrecv.at[base + i], device_id=to, device_id_type=MESH,
                )
            )
        table_pieces = pieces(table, 3)
        sent = sum(dot(send_hot, p) for p in table_pieces[::-1])
        return blocks, table_pieces, sent, copies

    def finish_send(sent, sb, rb, base):
        sb[0] = sent[:SP]
        sb[1] = sent[SP:]
        out = []
        for i, (src, dst, to) in enumerate(
            [(sb.at[0], rb.at[1], (lower, mp)), (sb.at[1], rb.at[0], (upper, mp))]
        ):
            out.append(
                pltpu.make_async_remote_copy(
                    src_ref=src, dst_ref=dst, send_sem=xsend.at[base + 2 + i],
                    recv_sem=xrecv.at[base + 2 + i], device_id=to, device_id_type=MESH,
                )
            )
        return out

    def plane_outside(own, rb, members, put):
        received = jnp.concatenate([rb[0], rb[1]], axis=0)
        got = own + right(hot_recv, received, 3)
        for a in range(2):
            for m in range(members):
                lanes = slice(FW * m, FW * (m + 1))
                lo = got[a * C : (a + 1) * C, lanes]
                hi = got[(2 + a) * C : (3 + a) * C, lanes]
                primal, tangent = swap(lo, hi)
                put(0, m, a, primal)
                put(1, m, a, tangent)

    def layer_outside(blocks, zr, members, put):
        step = (L - 1) * 32
        for m in range(members):
            lanes = slice(FW * m, FW * (m + 1))
            lo = jnp.where(
                flayer == 0,
                pltpu.roll(zr[0, :, lanes], (FW - step) % FW, 1),
                pltpu.roll(blocks[2][m][1], 32, 1),
            )
            hi = jnp.where(
                flayer == L - 1,
                pltpu.roll(zr[1, :, lanes], step, 1),
                pltpu.roll(blocks[2][m][0], FW - 32, 1),
            )
            primal, tangent = swap(lo, hi)
            put(0, m, 2, primal)
            put(1, m, 2, tangent)

    whole = u[...].reshape(10 * C, VW)
    for a in range(3):
        faces = left(whole, pick_ref[a], 3).reshape(2, 5, C, FW)
        for m in range(5):
            uf[0, m, a] = faces[0, m] + fpad if m % 4 == 0 else faces[0, m]
            uf[1, m, a] = faces[1, m]
    blocks1, table1, sent1, zcopies1 = exchange(
        lambda pt, m, a: uf[pt, m, a], 5, sb1, rb1, zs1, zr1, 0
    )
    pl.semaphore_wait(barrier, ns + np_ - 2)
    for copy in zcopies1:
        copy.start()
    pcopies1 = finish_send(sent1, sb1, rb1, 0)
    for copy in pcopies1:
        copy.start()

    own1 = sum(dot(hot_own, p) for p in table1[::-1])

    @pl.loop(0, C // 8)
    def _(i):
        rows = pl.ds(pl.multiple_of(i * 8, 8), 8)
        primal = [u[0, m, rows, :] for m in range(5)]
        tangent = [u[1, m, rows, :] for m in range(5)]
        fp, ft = jax.jvp(gradient_fields, (primal,), (tangent,))
        for m in range(4):
            w[0, m, rows, :] = fp[m]
            w[1, m, rows, :] = ft[m]

    fields = w[...].reshape(8 * C, VW)
    for a in range(3):
        q[a] = derive(fields, dh_ref[a], dl_ref[a]).reshape(2, 4, C, VW)

    for copy in zcopies1 + pcopies1:
        copy.wait()
    low_wall = jnp.where(fs_ref[:, 2:3] < 0, 1.0, 0.0)
    high_wall = jnp.where(fs_ref[:, 3:4] < 0, 1.0, 0.0)
    wall = jnp.where(first, low_wall, high_wall) > 0.5

    def put1(pt, m, a, value):
        if a == 1:
            own = uf[pt, m, a]
            value = jnp.where(wall, own if m % 4 == 0 else -own, value)
        of[pt, m, a] = value

    plane_outside(own1, rb1, 5, put1)
    layer_outside(blocks1, zr1, 5, put1)

    for a in range(3):
        @pl.loop(0, C // 8)
        def _(i):
            rows = pl.ds(pl.multiple_of(i * 8, 8), 8)
            primal = ([uf[0, m, a, rows, :] for m in range(5)], [of[0, m, a, rows, :] for m in range(5)])
            tangent = ([uf[1, m, a, rows, :] for m in range(5)], [of[1, m, a, rows, :] for m in range(5)])
            jp, jt = jax.jvp(jump_fields, primal, tangent)
            for m in range(4):
                jf[a, 0, m, rows, :] = (0.5 * LIFT) * sign * jp[m]
                jf[a, 1, m, rows, :] = (0.5 * LIFT) * sign * jt[m]

        q[a] += left(jf[a].reshape(8 * C, FW), lift_ref[a], 2).reshape(2, 4, C, VW)

    @pl.loop(0, C // 8)
    def _(i):
        rows = pl.ds(pl.multiple_of(i * 8, 8), 8)
        scale = [mv[a, rows, :] for a in range(3)]
        states = [[u[pt, m, rows, :] for m in range(5)] for pt in range(2)]
        grads = [
            [[scale[a] * q[a, pt, m, rows, :] for m in range(4)] for a in range(3)]
            for pt in range(2)
        ]
        vp, vt = jax.jvp(viscous_all, (states[0], grads[0]), (states[1], grads[1]))
        for a in range(3):
            for m in range(4):
                v[a, 0, m, rows, :] = vp[a][m]
                v[a, 1, m, rows, :] = vt[a][m]

    for a in range(3):
        vf[a] = left(v[a].reshape(8 * C, VW), pick_ref[a], 3).reshape(2, 4, C, FW)
    blocks2, table2, sent2, zcopies2 = exchange(
        lambda pt, m, a: vf[a, pt, m], 4, sb2, rb2, zs2, zr2, 4
    )
    for copy in zcopies2:
        copy.start()
    pcopies2 = finish_send(sent2, sb2, rb2, 4)
    for copy in pcopies2:
        copy.start()

    own2 = sum(dot(hot_own, p) for p in table2[::-1])

    @pl.loop(0, C // 8)
    def _(i):
        rows = pl.ds(pl.multiple_of(i * 8, 8), 8)
        states = [[u[pt, m, rows, :] for m in range(5)] for pt in range(2)]
        for a in range(3):
            scale = mv[a, rows, :]
            fluxes = jax.jvp(lambda x: inviscid(x, a), (states[0],), (states[1],))
            for pt in range(2):
                g[a, pt, 0, rows, :] = scale * fluxes[pt][0]
                for m in range(4):
                    g[a, pt, m + 1, rows, :] = scale * (fluxes[pt][m + 1] - v[a, pt, m, rows, :])

    for a in range(3):
        @pl.loop(0, C // 8)
        def _(i):
            rows = pl.ds(pl.multiple_of(i * 8, 8), 8)
            primal = ([uf[0, m, a, rows, :] for m in range(5)], [of[0, m, a, rows, :] for m in range(5)])
            tangent = ([uf[1, m, a, rows, :] for m in range(5)], [of[1, m, a, rows, :] for m in range(5)])
            sp, stt = jax.jvp(
                lambda inner, outer: surface(inner, outer, sign, a), primal, tangent
            )
            for m in range(5):
                s[a, 0, m, rows, :] = sp[m]
                s[a, 1, m, rows, :] = stt[m]

    total = None
    for a in range(3):
        part = derive(g[a].reshape(10 * C, VW), dh_ref[a], dl_ref[a])
        total = part if total is None else total + part
    r[...] = total.reshape(2, 5, C, VW)

    for copy in zcopies2 + pcopies2:
        copy.wait()

    def put2(pt, m, a, value):
        if a == 1:
            value = jnp.where(wall, vf[a, pt, m], value)
        ov[a, pt, m] = value

    plane_outside(own2, rb2, 4, put2)
    layer_outside(blocks2, zr2, 4, put2)
    lifted = None
    for a in range(3):
        for pt in range(2):
            s[a, pt, 0] = mf[a] * s[a, pt, 0]
            for m in range(4):
                jump = ov[a, pt, m] - vf[a, pt, m]
                s[a, pt, m + 1] = mf[a] * (s[a, pt, m + 1] - (0.5 * LIFT) * sign * jump)
        part = left(s[a].reshape(10 * C, FW), lift_ref[a], 2)
        lifted = part if lifted is None else lifted + part
    r[...] += lifted.reshape(2, 5, C, VW)

    def whole_sum(parts):
        acc = parts[0]
        for part in parts[1:]:
            acc = acc + part
        return jnp.sum(jnp.sum(acc, axis=0, keepdims=True), axis=1, keepdims=True)

    def ratio(top, bottom):
        return jnp.where(bottom > 0.0, top / jnp.where(bottom > 0.0, bottom, 1.0), 0.0)

    pd = whole_sum([r[1, m] * u[1, m] for m in range(5)])
    dd = whole_sum([u[1, m] * u[1, m] for m in range(5)])
    rs = whole_sum([r[0, m] * r[0, m] for m in range(5)])
    mine = ratio(pd, dd)
    rests = [r[1, m] - mine * u[1, m] for m in range(5)]
    rr = whole_sum([x * x for x in rests])
    rd = whole_sum([x * u[1, m] for m, x in enumerate(rests)])
    stats = [jnp.broadcast_to(x, (1, 128)) for x in (pd, dd, rs, rr, rd)]

    def write(stats):
        for i in range(5):
            st[i : i + 1, :] = stats[i]
        st[5:8, :] = jnp.zeros((3, 128), F32)

    def gathered(n, buf, ssem, rsem, peer):
        copies = []
        for k in range(1, n):
            copy = pltpu.make_async_remote_copy(
                src_ref=st, dst_ref=buf.at[k], send_sem=ssem.at[k], recv_sem=rsem.at[k],
                device_id=peer(k), device_id_type=MESH,
            )
            copy.start()
            copies.append(copy)
        buf[0] = st[...]
        for copy in copies:
            copy.wait()
        pd, dd, rs, rr, rd = [buf[:, i, :] for i in range(5)]
        own = ratio(pd, dd)
        add = lambda x: jnp.sum(x, axis=0, keepdims=True)
        pd0, dd0 = add(pd), add(dd)
        shift = own - ratio(pd0, dd0)
        rr0 = add(rr + 2.0 * shift * rd + shift * shift * dd)
        return [pd0, dd0, add(rs), rr0, add(rd + shift * dd)]

    write(stats)
    stats = gathered(np_, sta, asend, arecv, lambda k: (ms, lax.rem(mp + k, np_)))
    for l in range(L):
        for m in range(5):
            res_ref[:, l, 125 * m : 125 * (m + 1)] = r[0, m, :, 128 * l : 128 * l + 125]
    write(stats)
    pd, dd, rs, rr, rd = gathered(ns, stb, bsend, brecv, lambda k: (lax.rem(ms + k, ns), mp))
    coefficient = pd * (1.0 / total_count)
    shift = ratio(pd, dd) - coefficient
    beta = jnp.sqrt((rr + 2.0 * shift * rd + shift * shift * dd) * (1.0 / total_count))
    norm = jnp.sqrt(rs * (1.0 / total_count))
    lane = lax.broadcasted_iota(jnp.int32, (1, 128), 1)
    kry_ref[...] = jnp.where(lane == 0, coefficient, jnp.where(lane == 1, beta, norm))
    c, inv = coefficient[:, :1], 1.0 / beta[:, :1]
    for m in range(5):
        value = (r[1, m] - c * u[1, m]) * inv
        for l in range(L):
            basis_ref[:, l, 125 * m : 125 * (m + 1)] = value[:, 128 * l : 128 * l + 125]


def local(ns, np_, state, direction, metric, face_source, send_rows):
    C, L, width = state.shape
    slots = send_rows.shape[2]
    SP = -(-slots // 8) * 8
    VW, FW = 128 * L, 64 * L
    own = 4 * C
    keys = np.full((1, own + 2 * SP), -7, np.int32)
    side, rest = np.divmod(np.arange(own), 2 * C)
    keys[0, :own] = 4 * (rest % C) + 2 * (rest // C) + side
    keys[0, own : own + slots] = own + np.arange(slots)
    keys[0, own + SP : own + SP + slots] = own + slots + np.arange(slots)
    high, low, pick, lift = operators(L)
    vmem = lambda *shape: pltpu.VMEM(shape, F32)
    dma = lambda n: pltpu.SemaphoreType.DMA((n,))
    spec = pl.BlockSpec(memory_space=pltpu.VMEM)
    residual, basis, krylov = pl.pallas_call(
        functools.partial(kernel, ns, np_, float(state.size * ns * np_)),
        out_shape=(
            jax.ShapeDtypeStruct(state.shape, F32),
            jax.ShapeDtypeStruct(state.shape, F32),
            jax.ShapeDtypeStruct((1, 128), F32),
        ),
        in_specs=[spec] * 10,
        out_specs=(spec,) * 3,
        scratch_shapes=[
            vmem(2, 5, C, VW), vmem(2, 5, 3, C, FW), vmem(2, 5, 3, C, FW),
            vmem(2, 4, C, VW), vmem(3, 2, 4, C, FW), vmem(3, 2, 4, C, VW),
            vmem(3, 2, 4, C, VW), vmem(3, 2, 4, C, FW), vmem(3, 2, 4, C, FW),
            vmem(3, 2, 5, C, VW), vmem(3, 2, 5, C, FW), vmem(2, 5, C, VW),
            vmem(3, C, VW), vmem(3, C, FW),
            vmem(2, SP, 5 * FW), vmem(2, SP, 5 * FW), vmem(2, C, 5 * FW), vmem(2, C, 5 * FW),
            vmem(2, SP, 4 * FW), vmem(2, SP, 4 * FW), vmem(2, C, 4 * FW), vmem(2, C, 4 * FW),
            vmem(8, 128), vmem(np_, 8, 128), vmem(ns, 8, 128),
            dma(8), dma(8), dma(np_), dma(np_), dma(ns), dma(ns),
        ],
        compiler_params=pltpu.CompilerParams(
            collective_id=0, has_side_effects=True, vmem_limit_bytes=48 * 1024 * 1024
        ),
        name="navier",
    )(
        state, direction, metric, face_source, send_rows,
        jnp.asarray(keys), jnp.asarray(high), jnp.asarray(low), jnp.asarray(pick), jnp.asarray(lift),
    )
    return residual, basis, krylov[0, :3]


def solution(mesh):
    return jax.shard_map(
        functools.partial(local, mesh.shape["stream"], mesh.shape["span"]),
        mesh=mesh,
        in_specs=(
            P("stream", "span", None),
            P("stream", "span", None),
            P("stream", "span", None),
            P("stream", None),
            P("stream", None, None),
        ),
        out_specs=(P("stream", "span", None), P("stream", "span", None), P()),
        check_vma=False,
    )
```

profile of v0, /device:TPU:0, one launch (start us, length us, event | category | flops | bytes accessed | tf_op | source)
XLA Modules:
  0.0 39.4 jit_solution(9705037866006779012)
XLA Ops:
  0.6 0.0 copy-start.8
  0.6 0.8 %copy.14.fs_ref = s32[40,4]{1,0:T(8,128)S(1)} copy(s32[40,4]{0,1:T(4,128)} %param.13) | data formatting | bytes 1280 | tf_op args[3]
  1.4 0.0 copy-done.8
  1.4 0.0 copy-start.6
  1.4 0.0 copy-start.7
  1.4 0.1 copy.13.metric_ref
  1.5 0.6 %copy-done.6 = s32[1,2,33]{2,1,0:T(2,128)S(1)} copy-done((s32[1,2,33]{2,1,0:T(2,128)S(1)}, s32[1,2,33]{2,1,0:T(2,128)}, u32[]{:S(2)}) %copy-start.6) | copy-done | bytes 288
  2.1 0.0 copy-done.7
  2.1 0.0 copy-start
  2.1 1.0 %copy-done = bf16[3,256,256]{2,1,0:T(8,128)(2,1)S(1)} copy-done((bf16[3,256,256]{2,1,0:T(8,128)(2,1)S(1)}, bf16[3,256,256]{2,1,0:T(8,128)(2,1)}, u32[]{:S(2)}) %copy-start) | copy-done | bytes 393240
  3.1 0.0 copy-start.1
  3.1 1.0 %copy-done.1 = bf16[3,256,256]{2,1,0:T(8,128)(2,1)S(1)} copy-done((bf16[3,256,256]{2,1,0:T(8,128)(2,1)S(1)}, bf16[3,256,256]{2,1,0:T(8,128)(2,1)}, u32[]{:S(2)}) %copy-start.1) | copy-done | bytes 393240
  4.1 0.0 copy-start.2
  4.1 0.9 %copy-done.2 = f32[40,2,625]{2,1,0:T(2,128)S(1)} copy-done((f32[40,2,625]{2,1,0:T(2,128)S(1)}, f32[40,2,625]{2,1,0:T(2,128)}, u32[]{:S(2)}) %copy-start.2) | copy-done | bytes 200024
  5.0 0.0 copy-start.3
  5.0 0.9 %copy-done.3 = f32[40,2,625]{2,1,0:T(2,128)S(1)} copy-done((f32[40,2,625]{2,1,0:T(2,128)S(1)}, f32[40,2,625]{2,1,0:T(2,128)}, u32[]{:S(2)}) %copy-start.3) | copy-done | bytes 200024
  6.0 0.0 copy-start.4
  6.0 0.9 %copy-done.4 = bf16[3,128,256]{2,1,0:T(8,128)(2,1)S(1)} copy-done((bf16[3,128,256]{2,1,0:T(8,128)(2,1)S(1)}, bf16[3,128,256]{2,1,0:T(8,128)(2,1)}, u32[]{:S(2)}) %copy-start.4) | copy-done | bytes 196632
  6.9 0.0 copy-start.5
  6.9 0.9 %copy-done.5 = bf16[3,256,128]{2,1,0:T(8,128)(2,1)S(1)} copy-done((bf16[3,256,128]{2,1,0:T(8,128)(2,1)S(1)}, bf16[3,256,128]{2,1,0:T(8,128)(2,1)}, u32[]{:S(2)}) %copy-start.5) | copy-done | bytes 196632
  7.8 29.7 %navier.1 = (f32[40,2,625]{2,1,0:T(2,128)S(1)}, f32[40,2,625]{2,1,0:T(2,128)S(1)}, f32[1,128]{1,0:T(1,128)S(1)}) custom-call(f32[40,2,625]{2,1,0:T(2,128)S(1)} %copy-done.2, f32[40,2,625]{2,1,0:T(2,128)S(1)} %copy-done.3, f32[40,2,3]{2,1,0:T(2,128)S(1)} %copy.13.metric_ref, s32[40,4]{1,0:T(8,128)S(1)} %copy.14.fs_ref, s32[1,2,33]{2,1,0:T(2,128)S(1)} %copy-done.6, ...), custom_call_target="tpu_custom_call" | custom-call | tf_op jit(solution)/shard_map/navier/pallas_call | solution.py:510
  37.5 0.5 %slice_bitcast_fusion = f32[3]{0:T(128)} fusion(f32[1,128]{1,0:T(1,128)S(1)} %get-tuple-element.8), kind=kLoop, calls=%fused_computation | loop fusion | bytes 24 | tf_op jit(solution)/shard_map/squeeze | solution.py:538
  38.0 0.7 %copy.17 = f32[40,2,625]{2,1,0:T(2,128)} copy(f32[40,2,625]{2,1,0:T(2,128)S(1)} %get-tuple-element.12) | data formatting | bytes 400000
  38.7 0.7 %copy.18 = f32[40,2,625]{2,1,0:T(2,128)} copy(f32[40,2,625]{2,1,0:T(2,128)S(1)} %get-tuple-element.13) | data formatting | bytes 400000
Async XLA Ops:
  0.6 0.8 %copy-start.8 = (f32[40,2,3]{0,1,2:T(2,128)S(1)}, f32[40,2,3]{0,1,2:T(2,128)}, u32[]{:S(2)}) copy-start(f32[40,2,3]{0,1,2:T(2,128)} %param.12) | copy-start | bytes 2884
  1.4 0.7 %copy-start.6 = (s32[1,2,33]{2,1,0:T(2,128)S(1)}, s32[1,2,33]{2,1,0:T(2,128)}, u32[]{:S(2)}) copy-start(s32[1,2,33]{2,1,0:T(2,128)} %sr_ref.1) | copy-start | bytes 796
  1.4 0.7 %copy-start.7 = (s32[1,240]{1,0:T(1,128)S(1)}, s32[1,240]{1,0:T(1,128)}, u32[]{:S(2)}) copy-start(s32[1,240]{1,0:T(1,128)} %constant.10.clone.keyrow_ref) | copy-start | bytes 2884
  2.1 1.0 %copy-start = (bf16[3,256,256]{2,1,0:T(8,128)(2,1)S(1)}, bf16[3,256,256]{2,1,0:T(8,128)(2,1)}, u32[]{:S(2)}) copy-start(bf16[3,256,256]{2,1,0:T(8,128)(2,1)} %constant.12.clone.dl_ref) | copy-start | bytes 1179652
  3.1 1.0 %copy-start.1 = (bf16[3,256,256]{2,1,0:T(8,128)(2,1)S(1)}, bf16[3,256,256]{2,1,0:T(8,128)(2,1)}, u32[]{:S(2)}) copy-start(bf16[3,256,256]{2,1,0:T(8,128)(2,1)} %constant.11.clone.dh_ref) | copy-start | bytes 1179652
  4.1 0.9 %copy-start.2 = (f32[40,2,625]{2,1,0:T(2,128)S(1)}, f32[40,2,625]{2,1,0:T(2,128)}, u32[]{:S(2)}) copy-start(f32[40,2,625]{2,1,0:T(2,128)} %x_ref.1) | copy-start | bytes 600004
  5.0 0.9 %copy-start.3 = (f32[40,2,625]{2,1,0:T(2,128)S(1)}, f32[40,2,625]{2,1,0:T(2,128)}, u32[]{:S(2)}) copy-start(f32[40,2,625]{2,1,0:T(2,128)} %d_ref.1) | copy-start | bytes 600004
  6.0 0.9 %copy-start.4 = (bf16[3,128,256]{2,1,0:T(8,128)(2,1)S(1)}, bf16[3,128,256]{2,1,0:T(8,128)(2,1)}, u32[]{:S(2)}) copy-start(bf16[3,128,256]{2,1,0:T(8,128)(2,1)} %constant.14.clone.lift_ref) | copy-start | bytes 589828
  6.9 0.9 %copy-start.5 = (bf16[3,256,128]{2,1,0:T(8,128)(2,1)S(1)}, bf16[3,256,128]{2,1,0:T(8,128)(2,1)}, u32[]{:S(2)}) copy-start(bf16[3,256,128]{2,1,0:T(8,128)(2,1)} %constant.13.clone.pick_ref) | copy-start | bytes 589828
where the time goes:
time: 39.7 us; the launch traced here: 39.4 us
  Pallas kernels  29.7 us (75%)
  local copies, waits for them, and re-layouts  9.03 us (23%)
  between operations  0.66 us (2%)
    pallas_call x1, Pallas kernels, local(): pl.pallas_call(functools.partial(kernel, ns, np_, float(state.size * ns *...  29.7 us
    unnamed x22, local copies, waits for them, and re-layouts  8.52 us

commit v1 on v0

--- a/solution.py
+++ b/solution.py
@@ -142,11 +142,12 @@
 
 def kernel(
     ns, np_, total_count,
-    x_ref, d_ref, metric_ref, fs_ref, sr_ref, keyrow_ref, dh_ref, dl_ref, pick_ref, lift_ref,
+    x_hbm, d_hbm, metric_hbm, fs_hbm, sr_hbm, key_hbm, dh_hbm, dl_hbm, pick_hbm, lift_hbm,
     res_ref, basis_ref, kry_ref,
     u, uf, of, w, jf, q, v, vf, ov, g, s, r, mv, mf,
-    sb1, rb1, zs1, zr1, sb2, rb2, zs2, zr2, st, sta, stb,
-    xsend, xrecv, asend, arecv, bsend, brecv,
+    sb1, rb1, zs1, zr1, sb2, rb2, zs2, zr2, st, sta,
+    x_ref, d_ref, metric_ref, fs_ref, sr_ref, keyrow_ref, dh_ref, dl_ref, pick_ref, lift_ref,
+    xsend, xrecv, asend, arecv, loads,
 ):
     C, L = x_ref.shape[0], x_ref.shape[1]
     VW, FW, half = 128 * L, 64 * L, 32 * L
@@ -157,22 +158,48 @@
     lower, upper = lax.rem(ms + ns - 1, ns), lax.rem(ms + 1, ns)
     below, above = lax.rem(mp + np_ - 1, np_), lax.rem(mp + 1, np_)
 
+    inputs = [
+        pltpu.make_async_copy(src, dst, loads.at[i])
+        for i, (src, dst) in enumerate(
+            [
+                (x_hbm, x_ref), (d_hbm, d_ref), (pick_hbm, pick_ref), (key_hbm, keyrow_ref),
+                (fs_hbm, fs_ref), (sr_hbm, sr_ref), (metric_hbm, metric_ref),
+                (dh_hbm, dh_ref), (dl_hbm, dl_ref), (lift_hbm, lift_ref),
+            ]
+        )
+    ]
+    for copy in inputs:
+        copy.start()
+
+    def peer(k):
+        a, b = divmod(k, np_)
+        return lax.rem(ms + a, ns), lax.rem(mp + b, np_)
+
+    everyone = ns * np_
     barrier = pltpu.get_barrier_semaphore()
-    for k in range(1, ns):
-        pl.semaphore_signal(
-            barrier, inc=1, device_id=(lax.rem(ms + k, ns), mp), device_id_type=MESH
-        )
-    for k in range(1, np_):
-        pl.semaphore_signal(
-            barrier, inc=1, device_id=(ms, lax.rem(mp + k, np_)), device_id_type=MESH
-        )
+    for k in range(1, everyone):
+        pl.semaphore_signal(barrier, inc=1, device_id=peer(k), device_id_type=MESH)
 
     fl = lax.broadcasted_iota(jnp.int32, (1, FW), 1)
     vl = lax.broadcasted_iota(jnp.int32, (1, VW), 1)
     first = fl < half
     sign = jnp.where(first, -1.0, 1.0)
     flayer = lax.rem(fl, half) // 32
-    fpad = jnp.where(lax.rem(fl, 32) >= 25, 1.0, 0.0)
+    fnode = lax.rem(fl, 32)
+    fpad = jnp.where(fnode >= 25, 1.0, 0.0)
+
+    def roll(x, shift):
+        shift = shift % FW
+        return pltpu.roll(x, shift, 1) if shift else x
+
+    di = lax.broadcasted_iota(jnp.int32, (C, C), 0)
+    dj = lax.broadcasted_iota(jnp.int32, (C, C), 1)
+
+    def column(row):
+        return jnp.sum(jnp.where(di == dj, row, 0.0), axis=1, keepdims=True)
+
+    for copy in inputs[:2]:
+        copy.wait()
 
     for pt, ref in enumerate((x_ref, d_ref)):
         for l in range(L):
@@ -180,20 +207,13 @@
                 pad = 1.0 if pt == 0 and m % 4 == 0 else 0.0
                 u[pt, m, :, 128 * l + 120 : 128 * (l + 1)] = jnp.full((C, 8), pad, F32)
                 u[pt, m, :, 128 * l : 128 * l + 125] = ref[:, l, 125 * m : 125 * (m + 1)]
-    for a in range(3):
-        wide = jnp.zeros((C, VW), F32)
-        face = jnp.zeros((C, FW), F32)
-        for l in range(L):
-            value = metric_ref[:, l, a : a + 1]
-            wide = jnp.where(vl // 128 == l, value, wide)
-            face = jnp.where(flayer == l, value, face)
-        mv[a] = wide
-        mf[a] = face
-
-    keyrow = keyrow_ref[...]
+    for copy in inputs[2:7]:
+        copy.wait()
+    keyrow = keyrow_ref[...].astype(F32)
+    source = [column(fs_ref[f : f + 1, :].astype(F32)) for f in range(4)]
     onehot = jnp.concatenate(
         [
-            jnp.where(fs_ref[:, 2 * a + side : 2 * a + side + 1] == keyrow, 1.0, 0.0)
+            jnp.where(source[2 * a + side] == keyrow, 1.0, 0.0)
             for side in range(2)
             for a in range(2)
         ],
@@ -205,8 +225,8 @@
     send_hot = []
     for side in range(2):
         row = sr_ref[0, side : side + 1, :].astype(F32)
-        column = jnp.sum(jnp.where(ri == li, row, 0.0), axis=1, keepdims=True)
-        send_hot.append(jnp.where(column == keyrow[:, :OWN].astype(F32), 1.0, 0.0))
+        wanted = jnp.sum(jnp.where(ri == li, row, 0.0), axis=1, keepdims=True)
+        send_hot.append(jnp.where(wanted == keyrow[:, :OWN], 1.0, 0.0))
     send_hot = jnp.concatenate(send_hot, axis=0).astype(BF16)
 
     def swap(a, b):
@@ -225,9 +245,13 @@
             ],
             axis=0,
         )
-        for side in range(2):
-            for m in range(members):
-                zs[side, :, FW * m : FW * (m + 1)] = blocks[2][m][side]
+        for m in range(0, members, 2):
+            for side in range(2):
+                value = blocks[2][m][side]
+                if m + 1 < members:
+                    other = roll(blocks[2][m + 1][side], 32 if side == 0 else -32)
+                    value = jnp.where(flayer == (0 if side == 0 else L - 1), value, other)
+                zs[side, :, FW * (m // 2) : FW * (m // 2 + 1)] = value
         zs_copies = [
             (zs.at[0], zr.at[1], (ms, below)),
             (zs.at[1], zr.at[0], (ms, above)),
@@ -245,11 +269,20 @@
         return blocks, table_pieces, sent, copies
 
     def finish_send(sent, sb, rb, base):
-        sb[0] = sent[:SP]
-        sb[1] = sent[SP:]
+        width = sb.shape[2]
+        for m in range(width // FW):
+            value = sent[:, FW * m : FW * (m + 1)]
+            if sent.shape[1] > width:
+                spare = roll(sent[:, width:], 25 - 7 * m)
+                value = jnp.where(fnode < 25, value, spare)
+            sb[0, :, FW * m : FW * (m + 1)] = value[:SP]
+            sb[1, :, FW * m : FW * (m + 1)] = value[SP:]
         out = []
         for i, (src, dst, to) in enumerate(
-            [(sb.at[0], rb.at[1], (lower, mp)), (sb.at[1], rb.at[0], (upper, mp))]
+            [
+                (sb.at[0], rb.at[1], (lower, mp)),
+                (sb.at[1], rb.at[0], (upper, mp)),
+            ]
         ):
             out.append(
                 pltpu.make_async_remote_copy(
@@ -260,7 +293,16 @@
         return out
 
     def plane_outside(own, rb, members, put):
-        received = jnp.concatenate([rb[0], rb[1]], axis=0)
+        used = lax.broadcasted_iota(jnp.int32, (SP, 1), 0) < SLOTS
+        received = jnp.concatenate(
+            [jnp.where(used, rb[0], 0.0), jnp.where(used, rb[1], 0.0)], axis=0
+        )
+        if members * FW > received.shape[1]:
+            spare = jnp.zeros((2 * SP, FW), F32)
+            for m in range(received.shape[1] // FW):
+                part = roll(received[:, FW * m : FW * (m + 1)], 7 * m - 25)
+                spare = jnp.where((fnode >= 7 * m) & (fnode < 7 * m + 7), part, spare)
+            received = jnp.concatenate([received, spare], axis=1)
         got = own + right(hot_recv, received, 3)
         for a in range(2):
             for m in range(members):
@@ -272,19 +314,11 @@
                 put(1, m, a, tangent)
 
     def layer_outside(blocks, zr, members, put):
-        step = (L - 1) * 32
         for m in range(members):
-            lanes = slice(FW * m, FW * (m + 1))
-            lo = jnp.where(
-                flayer == 0,
-                pltpu.roll(zr[0, :, lanes], (FW - step) % FW, 1),
-                pltpu.roll(blocks[2][m][1], 32, 1),
-            )
-            hi = jnp.where(
-                flayer == L - 1,
-                pltpu.roll(zr[1, :, lanes], step, 1),
-                pltpu.roll(blocks[2][m][0], FW - 32, 1),
-            )
+            lanes = slice(FW * (m // 2), FW * (m // 2 + 1))
+            step = 32 * (L - 1 if m % 2 == 0 else L - 2)
+            lo = jnp.where(flayer == 0, roll(zr[0, :, lanes], -step), roll(blocks[2][m][1], 32))
+            hi = jnp.where(flayer == L - 1, roll(zr[1, :, lanes], step), roll(blocks[2][m][0], -32))
             primal, tangent = swap(lo, hi)
             put(0, m, 2, primal)
             put(1, m, 2, tangent)
@@ -298,12 +332,22 @@
     blocks1, table1, sent1, zcopies1 = exchange(
         lambda pt, m, a: uf[pt, m, a], 5, sb1, rb1, zs1, zr1, 0
     )
-    pl.semaphore_wait(barrier, ns + np_ - 2)
-    for copy in zcopies1:
+    pcopies1 = finish_send(sent1, sb1, rb1, 0)
+    pl.semaphore_wait(barrier, everyone - 1)
+    for copy in pcopies1 + zcopies1:
         copy.start()
-    pcopies1 = finish_send(sent1, sb1, rb1, 0)
-    for copy in pcopies1:
-        copy.start()
+    for a in range(3):
+        wide = jnp.zeros((C, VW), F32)
+        face = jnp.zeros((C, FW), F32)
+        for l in range(L):
+            value = column(metric_ref[a, l : l + 1, :])
+            wide = jnp.where(vl // 128 == l, value, wide)
+            face = jnp.where(flayer == l, value, face)
+        mv[a] = wide
+        mf[a] = face
+
+    for copy in inputs[7:]:
+        copy.wait()
 
     own1 = sum(dot(hot_own, p) for p in table1[::-1])
 
@@ -323,15 +367,15 @@
 
     for copy in zcopies1 + pcopies1:
         copy.wait()
-    low_wall = jnp.where(fs_ref[:, 2:3] < 0, 1.0, 0.0)
-    high_wall = jnp.where(fs_ref[:, 3:4] < 0, 1.0, 0.0)
+    low_wall = jnp.where(source[2] < 0.0, 1.0, 0.0)
+    high_wall = jnp.where(source[3] < 0.0, 1.0, 0.0)
     wall = jnp.where(first, low_wall, high_wall) > 0.5
 
     def put1(pt, m, a, value):
         if a == 1:
             own = uf[pt, m, a]
             value = jnp.where(wall, own if m % 4 == 0 else -own, value)
-        of[pt, m, a] = value
+        of[pt, m, a] = jnp.where(fnode < 25, value, uf[pt, m, a])
 
     plane_outside(own1, rb1, 5, put1)
     layer_outside(blocks1, zr1, 5, put1)
@@ -369,10 +413,8 @@
     blocks2, table2, sent2, zcopies2 = exchange(
         lambda pt, m, a: vf[a, pt, m], 4, sb2, rb2, zs2, zr2, 4
     )
-    for copy in zcopies2:
-        copy.start()
     pcopies2 = finish_send(sent2, sb2, rb2, 4)
-    for copy in pcopies2:
+    for copy in pcopies2 + zcopies2:
         copy.start()
 
     own2 = sum(dot(hot_own, p) for p in table2[::-1])
@@ -445,47 +487,38 @@
     rests = [r[1, m] - mine * u[1, m] for m in range(5)]
     rr = whole_sum([x * x for x in rests])
     rd = whole_sum([x * u[1, m] for m, x in enumerate(rests)])
-    stats = [jnp.broadcast_to(x, (1, 128)) for x in (pd, dd, rs, rr, rd)]
-
-    def write(stats):
-        for i in range(5):
-            st[i : i + 1, :] = stats[i]
-        st[5:8, :] = jnp.zeros((3, 128), F32)
-
-    def gathered(n, buf, ssem, rsem, peer):
-        copies = []
-        for k in range(1, n):
-            copy = pltpu.make_async_remote_copy(
-                src_ref=st, dst_ref=buf.at[k], send_sem=ssem.at[k], recv_sem=rsem.at[k],
-                device_id=peer(k), device_id_type=MESH,
-            )
-            copy.start()
-            copies.append(copy)
-        buf[0] = st[...]
-        for copy in copies:
-            copy.wait()
-        pd, dd, rs, rr, rd = [buf[:, i, :] for i in range(5)]
-        own = ratio(pd, dd)
-        add = lambda x: jnp.sum(x, axis=0, keepdims=True)
-        pd0, dd0 = add(pd), add(dd)
-        shift = own - ratio(pd0, dd0)
-        rr0 = add(rr + 2.0 * shift * rd + shift * shift * dd)
-        return [pd0, dd0, add(rs), rr0, add(rd + shift * dd)]
-
-    write(stats)
-    stats = gathered(np_, sta, asend, arecv, lambda k: (ms, lax.rem(mp + k, np_)))
+    lane = lax.broadcasted_iota(jnp.int32, (1, 128), 1)
+    row = jnp.zeros((1, 128), F32)
+    for i, value in enumerate((pd, dd, rs, rr, rd)):
+        row = jnp.where(lane == i, value, row)
+    st[...] = row
+    copies = [
+        pltpu.make_async_remote_copy(
+            src_ref=st, dst_ref=sta.at[k], send_sem=asend.at[k], recv_sem=arecv.at[k],
+            device_id=peer(k), device_id_type=MESH,
+        )
+        for k in range(1, everyone)
+    ]
+    for copy in copies:
+        copy.start()
+    sta[0] = st[...]
     for l in range(L):
         for m in range(5):
             res_ref[:, l, 125 * m : 125 * (m + 1)] = r[0, m, :, 128 * l : 128 * l + 125]
-    write(stats)
-    pd, dd, rs, rr, rd = gathered(ns, stb, bsend, brecv, lambda k: (lax.rem(ms + k, ns), mp))
-    coefficient = pd * (1.0 / total_count)
+    for copy in copies:
+        copy.wait()
+    table = sta[...].reshape(everyone, 128)
+    pd, dd, rs, rr, rd = [
+        jnp.sum(jnp.where(lane == i, table, 0.0), axis=1, keepdims=True) for i in range(5)
+    ]
+    coefficient = jnp.sum(pd, axis=0, keepdims=True) * (1.0 / total_count)
     shift = ratio(pd, dd) - coefficient
-    beta = jnp.sqrt((rr + 2.0 * shift * rd + shift * shift * dd) * (1.0 / total_count))
+    rr = jnp.sum(rr + 2.0 * shift * rd + shift * shift * dd, axis=0, keepdims=True)
+    rs = jnp.sum(rs, axis=0, keepdims=True)
+    beta = jnp.sqrt(rr * (1.0 / total_count))
     norm = jnp.sqrt(rs * (1.0 / total_count))
-    lane = lax.broadcasted_iota(jnp.int32, (1, 128), 1)
     kry_ref[...] = jnp.where(lane == 0, coefficient, jnp.where(lane == 1, beta, norm))
-    c, inv = coefficient[:, :1], 1.0 / beta[:, :1]
+    c, inv = coefficient, 1.0 / beta
     for m in range(5):
         value = (r[1, m] - c * u[1, m]) * inv
         for l in range(L):
@@ -504,6 +537,10 @@
     keys[0, own : own + slots] = own + np.arange(slots)
     keys[0, own + SP : own + SP + slots] = own + slots + np.arange(slots)
     high, low, pick, lift = operators(L)
+    operands = (
+        state, direction, jnp.transpose(metric, (2, 1, 0)), face_source.T, send_rows,
+        *[jnp.asarray(x) for x in (keys, high, low, pick, lift)],
+    )
     vmem = lambda *shape: pltpu.VMEM(shape, F32)
     dma = lambda n: pltpu.SemaphoreType.DMA((n,))
     spec = pl.BlockSpec(memory_space=pltpu.VMEM)
@@ -514,7 +551,7 @@
             jax.ShapeDtypeStruct(state.shape, F32),
             jax.ShapeDtypeStruct((1, 128), F32),
         ),
-        in_specs=[spec] * 10,
+        in_specs=[pl.BlockSpec(memory_space=pltpu.HBM)] * 10,
         out_specs=(spec,) * 3,
         scratch_shapes=[
             vmem(2, 5, C, VW), vmem(2, 5, 3, C, FW), vmem(2, 5, 3, C, FW),
@@ -522,19 +559,17 @@
             vmem(3, 2, 4, C, VW), vmem(3, 2, 4, C, FW), vmem(3, 2, 4, C, FW),
             vmem(3, 2, 5, C, VW), vmem(3, 2, 5, C, FW), vmem(2, 5, C, VW),
             vmem(3, C, VW), vmem(3, C, FW),
-            vmem(2, SP, 5 * FW), vmem(2, SP, 5 * FW), vmem(2, C, 5 * FW), vmem(2, C, 5 * FW),
-            vmem(2, SP, 4 * FW), vmem(2, SP, 4 * FW), vmem(2, C, 4 * FW), vmem(2, C, 4 * FW),
-            vmem(8, 128), vmem(np_, 8, 128), vmem(ns, 8, 128),
-            dma(8), dma(8), dma(np_), dma(np_), dma(ns), dma(ns),
+            vmem(2, SP, 4 * FW), vmem(2, SP, 4 * FW), vmem(2, C, 3 * FW), vmem(2, C, 3 * FW),
+            vmem(2, SP, 4 * FW), vmem(2, SP, 4 * FW), vmem(2, C, 2 * FW), vmem(2, C, 2 * FW),
+            vmem(1, 128), vmem(ns * np_, 1, 128),
+            *[pltpu.VMEM(x.shape, x.dtype) for x in operands],
+            dma(8), dma(8), dma(ns * np_), dma(ns * np_), dma(10),
         ],
         compiler_params=pltpu.CompilerParams(
-            collective_id=0, has_side_effects=True, vmem_limit_bytes=48 * 1024 * 1024
+            collective_id=0, has_side_effects=True, vmem_limit_bytes=40 * 1024 * 1024
         ),
         name="navier",
-    )(
-        state, direction, metric, face_source, send_rows,
-        jnp.asarray(keys), jnp.asarray(high), jnp.asarray(low), jnp.asarray(pick), jnp.asarray(lift),
-    )
+    )(*operands)
     return residual, basis, krylov[0, :3]
 
 

time: 39.7 us -> 39.6 us (level)
  Pallas kernels: 29.7 us -> 28.3 us
  local copies, waits for them, and re-layouts: 9.03 us -> 10.3 us
    pallas_call x1, Pallas kernels: 29.7 us -> 28.3 us  [local(): pl.pallas_call(functools.partial(kernel, ns, np_, float(state.size * ns *...]
    unnamed x22, local copies, waits for them, and re-layouts: 8.52 us -> 9.78 us
where the time goes in v1:
time: 39.6 us; the launch traced here: 39.2 us
  Pallas kernels  28.3 us (71%)
  local copies, waits for them, and re-layouts  10.3 us (26%)
  between operations  0.66 us (2%)
    pallas_call x1, Pallas kernels, local(): pl.pallas_call(functools.partial(kernel, ns, np_, float(state.size * ns *...  28.3 us
    unnamed x22, local copies, waits for them, and re-layouts  9.78 us

profile of v1, /device:TPU:0, one launch (start us, length us, event | category | flops | bytes accessed | tf_op | source)
XLA Modules:
  0.0 39.2 jit_solution(10811585541699633521)
XLA Ops:
  0.6 0.0 copy-start.6
  0.6 0.7 %copy-done.6 = f32[40,2,3]{0,1,2:T(2,128)S(1)} copy-done((f32[40,2,3]{0,1,2:T(2,128)S(1)}, f32[40,2,3]{0,1,2:T(2,128)}, u32[]{:S(2)}) %copy-start.6) | copy-done | bytes 984
  1.3 0.0 copy-start
  1.3 1.0 %copy-done = bf16[3,256,256]{2,1,0:T(8,128)(2,1)S(1)} copy-done((bf16[3,256,256]{2,1,0:T(8,128)(2,1)S(1)}, bf16[3,256,256]{2,1,0:T(8,128)(2,1)}, u32[]{:S(2)}) %copy-start) | copy-done | bytes 393240
  2.3 0.0 copy-start.1
  2.3 1.0 %copy-done.1 = bf16[3,256,256]{2,1,0:T(8,128)(2,1)S(1)} copy-done((bf16[3,256,256]{2,1,0:T(8,128)(2,1)S(1)}, bf16[3,256,256]{2,1,0:T(8,128)(2,1)}, u32[]{:S(2)}) %copy-start.1) | copy-done | bytes 393240
  3.3 0.0 copy-start.2
  3.3 0.9 %copy-done.2 = f32[40,2,625]{2,1,0:T(2,128)S(1)} copy-done((f32[40,2,625]{2,1,0:T(2,128)S(1)}, f32[40,2,625]{2,1,0:T(2,128)}, u32[]{:S(2)}) %copy-start.2) | copy-done | bytes 200024
  4.2 0.0 copy-start.3
  4.2 0.9 %copy-done.3 = f32[40,2,625]{2,1,0:T(2,128)S(1)} copy-done((f32[40,2,625]{2,1,0:T(2,128)S(1)}, f32[40,2,625]{2,1,0:T(2,128)}, u32[]{:S(2)}) %copy-start.3) | copy-done | bytes 200024
  5.2 0.0 copy-start.4
  5.2 0.9 %copy-done.4 = bf16[3,128,256]{2,1,0:T(8,128)(2,1)S(1)} copy-done((bf16[3,128,256]{2,1,0:T(8,128)(2,1)S(1)}, bf16[3,128,256]{2,1,0:T(8,128)(2,1)}, u32[]{:S(2)}) %copy-start.4) | copy-done | bytes 196632
  6.1 0.0 copy-start.5
  6.1 0.9 %copy-done.5 = bf16[3,256,128]{2,1,0:T(8,128)(2,1)S(1)} copy-done((bf16[3,256,128]{2,1,0:T(8,128)(2,1)S(1)}, bf16[3,256,128]{2,1,0:T(8,128)(2,1)}, u32[]{:S(2)}) %copy-start.5) | copy-done | bytes 196632
  7.0 0.0 copy-start.7
  7.0 0.7 %copy-done.7 = s32[40,4]{0,1:T(4,128)S(1)} copy-done((s32[40,4]{0,1:T(4,128)S(1)}, s32[40,4]{0,1:T(4,128)}, u32[]{:S(2)}) %copy-start.7) | copy-done | bytes 664
  7.7 0.0 copy-start.8
  7.7 0.7 %copy-done.8 = s32[1,2,33]{2,1,0:T(2,128)S(1)} copy-done((s32[1,2,33]{2,1,0:T(2,128)S(1)}, s32[1,2,33]{2,1,0:T(2,128)}, u32[]{:S(2)}) %copy-start.8) | copy-done | bytes 288
  8.4 0.0 copy-start.9
  8.4 0.7 %copy-done.9 = s32[1,240]{1,0:T(1,128)S(1)} copy-done((s32[1,240]{1,0:T(1,128)S(1)}, s32[1,240]{1,0:T(1,128)}, u32[]{:S(2)}) %copy-start.9) | copy-done | bytes 984
  9.1 28.3 %navier.1 = (f32[40,2,625]{2,1,0:T(2,128)S(1)}, f32[40,2,625]{2,1,0:T(2,128)S(1)}, f32[1,128]{1,0:T(1,128)S(1)}) custom-call(f32[40,2,625]{2,1,0:T(2,128)S(1)} %copy-done.2, f32[40,2,625]{2,1,0:T(2,128)S(1)} %copy-done.3, f32[3,2,40]{2,1,0:T(2,128)S(1)} %bitcast.4, s32[4,40]{1,0:T(4,128)S(1)} %bitcast.5, s32[1,2,33]{2,1,0:T(2,128)S(1)} %copy-done.8, ...), custom_call_target="tpu_custom_call" | custom-call | tf_op jit(solution)/shard_map/navier/pallas_call | solution.py:547
  37.3 0.5 %slice_bitcast_fusion = f32[3]{0:T(128)} fusion(f32[1,128]{1,0:T(1,128)S(1)} %get-tuple-element.8), kind=kLoop, calls=%fused_computation | loop fusion | bytes 24 | tf_op jit(solution)/shard_map/squeeze | solution.py:573
  37.9 0.7 %copy.15 = f32[40,2,625]{2,1,0:T(2,128)} copy(f32[40,2,625]{2,1,0:T(2,128)S(1)} %get-tuple-element.12) | data formatting | bytes 400000
  38.5 0.7 %copy.16 = f32[40,2,625]{2,1,0:T(2,128)} copy(f32[40,2,625]{2,1,0:T(2,128)S(1)} %get-tuple-element.13) | data formatting | bytes 400000
Async XLA Ops:
  0.6 0.7 %copy-start.6 = (f32[40,2,3]{0,1,2:T(2,128)S(1)}, f32[40,2,3]{0,1,2:T(2,128)}, u32[]{:S(2)}) copy-start(f32[40,2,3]{0,1,2:T(2,128)} %param.12) | copy-start | bytes 2884
  1.3 1.0 %copy-start = (bf16[3,256,256]{2,1,0:T(8,128)(2,1)S(1)}, bf16[3,256,256]{2,1,0:T(8,128)(2,1)}, u32[]{:S(2)}) copy-start(bf16[3,256,256]{2,1,0:T(8,128)(2,1)} %constant.12.clone.dl_hbm) | copy-start | bytes 1179652
  2.3 1.0 %copy-start.1 = (bf16[3,256,256]{2,1,0:T(8,128)(2,1)S(1)}, bf16[3,256,256]{2,1,0:T(8,128)(2,1)}, u32[]{:S(2)}) copy-start(bf16[3,256,256]{2,1,0:T(8,128)(2,1)} %constant.11.clone.dh_hbm) | copy-start | bytes 1179652
  3.3 0.9 %copy-start.2 = (f32[40,2,625]{2,1,0:T(2,128)S(1)}, f32[40,2,625]{2,1,0:T(2,128)}, u32[]{:S(2)}) copy-start(f32[40,2,625]{2,1,0:T(2,128)} %x_hbm.1) | copy-start | bytes 600004
  4.2 0.9 %copy-start.3 = (f32[40,2,625]{2,1,0:T(2,128)S(1)}, f32[40,2,625]{2,1,0:T(2,128)}, u32[]{:S(2)}) copy-start(f32[40,2,625]{2,1,0:T(2,128)} %d_hbm.1) | copy-start | bytes 600004
  5.2 0.9 %copy-start.4 = (bf16[3,128,256]{2,1,0:T(8,128)(2,1)S(1)}, bf16[3,128,256]{2,1,0:T(8,128)(2,1)}, u32[]{:S(2)}) copy-start(bf16[3,128,256]{2,1,0:T(8,128)(2,1)} %constant.14.clone.lift_hbm) | copy-start | bytes 589828
  6.1 0.9 %copy-start.5 = (bf16[3,256,128]{2,1,0:T(8,128)(2,1)S(1)}, bf16[3,256,128]{2,1,0:T(8,128)(2,1)}, u32[]{:S(2)}) copy-start(bf16[3,256,128]{2,1,0:T(8,128)(2,1)} %constant.13.clone.pick_hbm) | copy-start | bytes 589828
  7.0 0.7 %copy-start.7 = (s32[40,4]{0,1:T(4,128)S(1)}, s32[40,4]{0,1:T(4,128)}, u32[]{:S(2)}) copy-start(s32[40,4]{0,1:T(4,128)} %param.13) | copy-start | bytes 1924
  7.7 0.7 %copy-start.8 = (s32[1,2,33]{2,1,0:T(2,128)S(1)}, s32[1,2,33]{2,1,0:T(2,128)}, u32[]{:S(2)}) copy-start(s32[1,2,33]{2,1,0:T(2,128)} %sr_hbm.1) | copy-start | bytes 796
  8.4 0.7 %copy-start.9 = (s32[1,240]{1,0:T(1,128)S(1)}, s32[1,240]{1,0:T(1,128)}, u32[]{:S(2)}) copy-start(s32[1,240]{1,0:T(1,128)} %constant.10.clone.key_hbm) | copy-start | bytes 2884

commit v2 on v1

--- a/solution.py
+++ b/solution.py
@@ -566,7 +566,7 @@
             dma(8), dma(8), dma(ns * np_), dma(ns * np_), dma(10),
         ],
         compiler_params=pltpu.CompilerParams(
-            collective_id=0, has_side_effects=True, vmem_limit_bytes=40 * 1024 * 1024
+            collective_id=0, has_side_effects=True, vmem_limit_bytes=63 * 1024 * 1024
         ),
         name="navier",
     )(*operands)

time: 39.6 us -> 32.7 us (0.83)
  local copies, waits for them, and re-layouts: 10.3 us -> 3.54 us
    unnamed x22 -> x6, local copies, waits for them, and re-layouts: 9.78 us -> 3.03 us
where the time goes in v2:
time: 32.7 us; the launch traced here: 32.5 us
  Pallas kernels  28.4 us (87%)
  local copies, waits for them, and re-layouts  3.54 us (11%)
  between operations  0.65 us (2%)
    pallas_call x1, Pallas kernels, local(): pl.pallas_call(functools.partial(kernel, ns, np_, float(state.size * ns *...  28.4 us
    unnamed x6, local copies, waits for them, and re-layouts  3.03 us

profile of v2, /device:TPU:0, one launch (start us, length us, event | category | flops | bytes accessed | tf_op | source)
XLA Modules:
  0.0 32.5 jit_solution(14555575782752724219)
XLA Ops:
  0.6 28.4 %navier.1 = (f32[40,2,625]{2,1,0:T(2,128)}, f32[40,2,625]{2,1,0:T(2,128)}, f32[1,128]{1,0:T(1,128)}) custom-call(f32[40,2,625]{2,1,0:T(2,128)} %x_hbm.1, f32[40,2,625]{2,1,0:T(2,128)} %d_hbm.1, f32[3,2,40]{2,1,0:T(2,128)} %bitcast.4, s32[4,40]{1,0:T(4,128)} %bitcast.5, s32[1,2,33]{2,1,0:T(2,128)} %sr_hbm.1, s32[1,240]{1,0:T(1,128)} %constant.10.clone.key_hbm, ...), custom_call_target="tpu_custom_call" | custom-call | tf_op jit(solution)/shard_map/navier/pallas_call | solution.py:547
  29.0 0.0 copy-start.1
  29.0 0.7 %copy-done.1 = f32[1,128]{1,0:T(1,128)S(1)} copy-done((f32[1,128]{1,0:T(1,128)S(1)}, f32[1,128]{1,0:T(1,128)}, u32[]{:S(2)}) %copy-start.1) | copy-done | bytes 536
  29.7 0.5 %slice_bitcast_fusion = f32[3]{0:T(128)} fusion(f32[1,128]{1,0:T(1,128)S(1)} %copy-done.1), kind=kLoop, calls=%fused_computation | loop fusion | bytes 24 | tf_op jit(solution)/shard_map/squeeze | solution.py:573
  30.2 0.0 copy-start
  30.2 1.7 %copy.15 = f32[40,2,625]{2,1,0:T(2,128)} copy(f32[40,2,625]{2,1,0:T(2,128)} %get-tuple-element.12) | data formatting | bytes 400000
  31.9 0.0 copy-done
  31.9 0.7 %copy.16 = f32[40,2,625]{2,1,0:T(2,128)} copy(f32[40,2,625]{2,1,0:T(2,128)S(1)} %copy-done) | data formatting | bytes 400000
Async XLA Ops:
  29.0 0.7 %copy-start.1 = (f32[1,128]{1,0:T(1,128)S(1)}, f32[1,128]{1,0:T(1,128)}, u32[]{:S(2)}) copy-start(f32[1,128]{1,0:T(1,128)} %get-tuple-element.8) | copy-start | bytes 1540
  30.2 1.7 %copy-start = (f32[40,2,625]{2,1,0:T(2,128)S(1)}, f32[40,2,625]{2,1,0:T(2,128)}, u32[]{:S(2)}) copy-start(f32[40,2,625]{2,1,0:T(2,128)} %get-tuple-element.13) | copy-start | bytes 600004

commit v3 on v2

--- a/solution.py
+++ b/solution.py
@@ -152,7 +152,8 @@
     C, L = x_ref.shape[0], x_ref.shape[1]
     VW, FW, half = 128 * L, 64 * L, 32 * L
     SLOTS = sr_ref.shape[2]
-    SP = sb1.shape[1]
+    SP = -(-SLOTS // 8) * 8
+    MAIN, REM = SLOTS // 8, SLOTS % 8
     OWN = 4 * C
     ms, mp = lax.axis_index("stream"), lax.axis_index("span")
     lower, upper = lax.rem(ms + ns - 1, ns), lax.rem(ms + 1, ns)
@@ -269,14 +270,18 @@
         return blocks, table_pieces, sent, copies
 
     def finish_send(sent, sb, rb, base):
-        width = sb.shape[2]
-        for m in range(width // FW):
+        for m in range(4):
             value = sent[:, FW * m : FW * (m + 1)]
-            if sent.shape[1] > width:
-                spare = roll(sent[:, width:], 25 - 7 * m)
+            if sent.shape[1] > 4 * FW:
+                spare = roll(sent[:, 4 * FW :], 25 - 7 * m)
                 value = jnp.where(fnode < 25, value, spare)
-            sb[0, :, FW * m : FW * (m + 1)] = value[:SP]
-            sb[1, :, FW * m : FW * (m + 1)] = value[SP:]
+            for side in range(2):
+                for b in range(MAIN):
+                    at = side * SP + 8 * b
+                    sb[side, 4 * b + m] = value[at : at + 8]
+                for e in range(REM):
+                    at, to = side * SP + 8 * MAIN + e, REM * m + e
+                    sb[side, 4 * MAIN + to // 8, to % 8 : to % 8 + 1, :] = value[at : at + 1]
         out = []
         for i, (src, dst, to) in enumerate(
             [
@@ -293,10 +298,24 @@
         return out
 
     def plane_outside(own, rb, members, put):
-        used = lax.broadcasted_iota(jnp.int32, (SP, 1), 0) < SLOTS
-        received = jnp.concatenate(
-            [jnp.where(used, rb[0], 0.0), jnp.where(used, rb[1], 0.0)], axis=0
-        )
+        row8 = lax.broadcasted_iota(jnp.int32, (8, 1), 0)
+        rows = []
+        for side in range(2):
+            rows += [
+                jnp.concatenate([rb[side, 4 * b + m] for m in range(4)], axis=1)
+                for b in range(MAIN)
+            ]
+            if REM:
+                parts = []
+                for m in range(4):
+                    part = jnp.zeros((8, FW), F32)
+                    for e in range(REM):
+                        to = REM * m + e
+                        line = rb[side, 4 * MAIN + to // 8, to % 8 : to % 8 + 1, :]
+                        part = jnp.where(row8 == e, line, part)
+                    parts.append(part)
+                rows.append(jnp.concatenate(parts, axis=1))
+        received = jnp.concatenate(rows, axis=0)
         if members * FW > received.shape[1]:
             spare = jnp.zeros((2 * SP, FW), F32)
             for m in range(received.shape[1] // FW):
@@ -351,7 +370,7 @@
 
     own1 = sum(dot(hot_own, p) for p in table1[::-1])
 
-    @pl.loop(0, C // 8)
+    @pl.loop(0, C // 8, unroll=True)
     def _(i):
         rows = pl.ds(pl.multiple_of(i * 8, 8), 8)
         primal = [u[0, m, rows, :] for m in range(5)]
@@ -381,7 +400,7 @@
     layer_outside(blocks1, zr1, 5, put1)
 
     for a in range(3):
-        @pl.loop(0, C // 8)
+        @pl.loop(0, C // 8, unroll=True)
         def _(i):
             rows = pl.ds(pl.multiple_of(i * 8, 8), 8)
             primal = ([uf[0, m, a, rows, :] for m in range(5)], [of[0, m, a, rows, :] for m in range(5)])
@@ -393,7 +412,7 @@
 
         q[a] += left(jf[a].reshape(8 * C, FW), lift_ref[a], 2).reshape(2, 4, C, VW)
 
-    @pl.loop(0, C // 8)
+    @pl.loop(0, C // 8, unroll=True)
     def _(i):
         rows = pl.ds(pl.multiple_of(i * 8, 8), 8)
         scale = [mv[a, rows, :] for a in range(3)]
@@ -419,7 +438,7 @@
 
     own2 = sum(dot(hot_own, p) for p in table2[::-1])
 
-    @pl.loop(0, C // 8)
+    @pl.loop(0, C // 8, unroll=True)
     def _(i):
         rows = pl.ds(pl.multiple_of(i * 8, 8), 8)
         states = [[u[pt, m, rows, :] for m in range(5)] for pt in range(2)]
@@ -432,7 +451,7 @@
                     g[a, pt, m + 1, rows, :] = scale * (fluxes[pt][m + 1] - v[a, pt, m, rows, :])
 
     for a in range(3):
-        @pl.loop(0, C // 8)
+        @pl.loop(0, C // 8, unroll=True)
         def _(i):
             rows = pl.ds(pl.multiple_of(i * 8, 8), 8)
             primal = ([uf[0, m, a, rows, :] for m in range(5)], [of[0, m, a, rows, :] for m in range(5)])
@@ -536,6 +555,7 @@
     keys[0, :own] = 4 * (rest % C) + 2 * (rest // C) + side
     keys[0, own : own + slots] = own + np.arange(slots)
     keys[0, own + SP : own + SP + slots] = own + slots + np.arange(slots)
+    tiles = 4 * (slots // 8) + -(-4 * (slots % 8) // 8)
     high, low, pick, lift = operators(L)
     operands = (
         state, direction, jnp.transpose(metric, (2, 1, 0)), face_source.T, send_rows,
@@ -559,8 +579,8 @@
             vmem(3, 2, 4, C, VW), vmem(3, 2, 4, C, FW), vmem(3, 2, 4, C, FW),
             vmem(3, 2, 5, C, VW), vmem(3, 2, 5, C, FW), vmem(2, 5, C, VW),
             vmem(3, C, VW), vmem(3, C, FW),
-            vmem(2, SP, 4 * FW), vmem(2, SP, 4 * FW), vmem(2, C, 3 * FW), vmem(2, C, 3 * FW),
-            vmem(2, SP, 4 * FW), vmem(2, SP, 4 * FW), vmem(2, C, 2 * FW), vmem(2, C, 2 * FW),
+            vmem(2, tiles, 8, FW), vmem(2, tiles, 8, FW), vmem(2, C, 3 * FW), vmem(2, C, 3 * FW),
+            vmem(2, tiles, 8, FW), vmem(2, tiles, 8, FW), vmem(2, C, 2 * FW), vmem(2, C, 2 * FW),
             vmem(1, 128), vmem(ns * np_, 1, 128),
             *[pltpu.VMEM(x.shape, x.dtype) for x in operands],
             dma(8), dma(8), dma(ns * np_), dma(ns * np_), dma(10),

time: 32.7 us -> 31 us (0.948)
  Pallas kernels: 28.4 us -> 26.7 us
    pallas_call x1, Pallas kernels: 28.4 us -> 26.7 us  [local(): pl.pallas_call(functools.partial(kernel, ns, np_, float(state.size * ns *...]
where the time goes in v3:
time: 31 us; the launch traced here: 30.9 us
  Pallas kernels  26.7 us (86%)
  local copies, waits for them, and re-layouts  3.54 us (11%)
  between operations  0.65 us (2%)
    pallas_call x1, Pallas kernels, local(): pl.pallas_call(functools.partial(kernel, ns, np_, float(state.size * ns *...  26.7 us
    unnamed x6, local copies, waits for them, and re-layouts  3.03 us

profile of v3, /device:TPU:0, one launch (start us, length us, event | category | flops | bytes accessed | tf_op | source)
XLA Modules:
  0.0 30.9 jit_solution(4422723549546148287)
XLA Ops:
  0.6 26.7 %navier.1 = (f32[40,2,625]{2,1,0:T(2,128)}, f32[40,2,625]{2,1,0:T(2,128)}, f32[1,128]{1,0:T(1,128)}) custom-call(f32[40,2,625]{2,1,0:T(2,128)} %x_hbm.1, f32[40,2,625]{2,1,0:T(2,128)} %d_hbm.1, f32[3,2,40]{2,1,0:T(2,128)} %bitcast.4, s32[4,40]{1,0:T(4,128)} %bitcast.5, s32[1,2,33]{2,1,0:T(2,128)} %sr_hbm.1, s32[1,240]{1,0:T(1,128)} %constant.10.clone.key_hbm, ...), custom_call_target="tpu_custom_call" | custom-call | tf_op jit(solution)/shard_map/navier/pallas_call | solution.py:567
  27.3 0.0 copy-start.1
  27.3 0.7 %copy-done.1 = f32[1,128]{1,0:T(1,128)S(1)} copy-done((f32[1,128]{1,0:T(1,128)S(1)}, f32[1,128]{1,0:T(1,128)}, u32[]{:S(2)}) %copy-start.1) | copy-done | bytes 536
  28.0 0.5 %slice_bitcast_fusion = f32[3]{0:T(128)} fusion(f32[1,128]{1,0:T(1,128)S(1)} %copy-done.1), kind=kLoop, calls=%fused_computation | loop fusion | bytes 24 | tf_op jit(solution)/shard_map/squeeze | solution.py:593
  28.5 0.0 copy-start
  28.5 1.7 %copy.15 = f32[40,2,625]{2,1,0:T(2,128)} copy(f32[40,2,625]{2,1,0:T(2,128)} %get-tuple-element.12) | data formatting | bytes 400000
  30.2 0.0 copy-done
  30.2 0.7 %copy.16 = f32[40,2,625]{2,1,0:T(2,128)} copy(f32[40,2,625]{2,1,0:T(2,128)S(1)} %copy-done) | data formatting | bytes 400000
Async XLA Ops:
  27.3 0.7 %copy-start.1 = (f32[1,128]{1,0:T(1,128)S(1)}, f32[1,128]{1,0:T(1,128)}, u32[]{:S(2)}) copy-start(f32[1,128]{1,0:T(1,128)} %get-tuple-element.8) | copy-start | bytes 1540
  28.5 1.7 %copy-start = (f32[40,2,625]{2,1,0:T(2,128)S(1)}, f32[40,2,625]{2,1,0:T(2,128)}, u32[]{:S(2)}) copy-start(f32[40,2,625]{2,1,0:T(2,128)} %get-tuple-element.13) | copy-start | bytes 600004

commit v4 on v3

--- a/solution.py
+++ b/solution.py
@@ -140,14 +140,18 @@
     ]
 
 
+def ratio(top, bottom):
+    return jnp.where(bottom > 0.0, top / jnp.where(bottom > 0.0, bottom, 1.0), 0.0)
+
+
 def kernel(
-    ns, np_, total_count,
+    ns, np_,
     x_hbm, d_hbm, metric_hbm, fs_hbm, sr_hbm, key_hbm, dh_hbm, dl_hbm, pick_hbm, lift_hbm,
-    res_ref, basis_ref, kry_ref,
+    r_hbm, table_ref,
     u, uf, of, w, jf, q, v, vf, ov, g, s, r, mv, mf,
     sb1, rb1, zs1, zr1, sb2, rb2, zs2, zr2, st, sta,
     x_ref, d_ref, metric_ref, fs_ref, sr_ref, keyrow_ref, dh_ref, dl_ref, pick_ref, lift_ref,
-    xsend, xrecv, asend, arecv, loads,
+    xsend, xrecv, asend, arecv, loads, store,
 ):
     C, L = x_ref.shape[0], x_ref.shape[1]
     VW, FW, half = 128 * L, 64 * L, 32 * L
@@ -490,14 +494,14 @@
         lifted = part if lifted is None else lifted + part
     r[...] += lifted.reshape(2, 5, C, VW)
 
+    writing = pltpu.make_async_copy(r, r_hbm, store.at[0])
+    writing.start()
+
     def whole_sum(parts):
         acc = parts[0]
         for part in parts[1:]:
             acc = acc + part
         return jnp.sum(jnp.sum(acc, axis=0, keepdims=True), axis=1, keepdims=True)
-
-    def ratio(top, bottom):
-        return jnp.where(bottom > 0.0, top / jnp.where(bottom > 0.0, bottom, 1.0), 0.0)
 
     pd = whole_sum([r[1, m] * u[1, m] for m in range(5)])
     dd = whole_sum([u[1, m] * u[1, m] for m in range(5)])
@@ -521,12 +525,32 @@
     for copy in copies:
         copy.start()
     sta[0] = st[...]
+    for copy in copies:
+        copy.wait()
+    table_ref[...] = sta[...].reshape(everyone, 128)
+    writing.wait()
+
+
+def finish(
+    total_count, r_hbm, d_hbm, table_hbm, res_hbm, basis_hbm, kry_ref, r, d, table_ref, res, basis, sems
+):
+    C, L = d.shape[0], d.shape[1]
+    loads = [
+        pltpu.make_async_copy(src, dst, sems.at[i])
+        for i, (src, dst) in enumerate([(r_hbm, r), (d_hbm, d), (table_hbm, table_ref)])
+    ]
+    for copy in loads:
+        copy.start()
+    loads[0].wait()
     for l in range(L):
         for m in range(5):
-            res_ref[:, l, 125 * m : 125 * (m + 1)] = r[0, m, :, 128 * l : 128 * l + 125]
-    for copy in copies:
+            res[:, l, 125 * m : 125 * (m + 1)] = r[0, m, :, 128 * l : 128 * l + 125]
+    first = pltpu.make_async_copy(res, res_hbm, sems.at[3])
+    first.start()
+    for copy in loads[1:]:
         copy.wait()
-    table = sta[...].reshape(everyone, 128)
+    lane = lax.broadcasted_iota(jnp.int32, (1, 128), 1)
+    table = table_ref[...]
     pd, dd, rs, rr, rd = [
         jnp.sum(jnp.where(lane == i, table, 0.0), axis=1, keepdims=True) for i in range(5)
     ]
@@ -536,12 +560,18 @@
     rs = jnp.sum(rs, axis=0, keepdims=True)
     beta = jnp.sqrt(rr * (1.0 / total_count))
     norm = jnp.sqrt(rs * (1.0 / total_count))
-    kry_ref[...] = jnp.where(lane == 0, coefficient, jnp.where(lane == 1, beta, norm))
+    row = jnp.where(lane == 0, coefficient, jnp.where(lane == 1, beta, norm))
+    kry_ref[...] = row[0, :3]
     c, inv = coefficient, 1.0 / beta
-    for m in range(5):
-        value = (r[1, m] - c * u[1, m]) * inv
-        for l in range(L):
-            basis_ref[:, l, 125 * m : 125 * (m + 1)] = value[:, 128 * l : 128 * l + 125]
+    for l in range(L):
+        for m in range(5):
+            at = slice(125 * m, 125 * (m + 1))
+            product = r[1, m, :, 128 * l : 128 * l + 125]
+            basis[:, l, at] = (product - c * d[:, l, at]) * inv
+    second = pltpu.make_async_copy(basis, basis_hbm, sems.at[4])
+    second.start()
+    first.wait()
+    second.wait()
 
 
 def local(ns, np_, state, direction, metric, face_source, send_rows):
@@ -564,15 +594,14 @@
     vmem = lambda *shape: pltpu.VMEM(shape, F32)
     dma = lambda n: pltpu.SemaphoreType.DMA((n,))
     spec = pl.BlockSpec(memory_space=pltpu.VMEM)
-    residual, basis, krylov = pl.pallas_call(
-        functools.partial(kernel, ns, np_, float(state.size * ns * np_)),
+    parts, table = pl.pallas_call(
+        functools.partial(kernel, ns, np_),
         out_shape=(
-            jax.ShapeDtypeStruct(state.shape, F32),
-            jax.ShapeDtypeStruct(state.shape, F32),
-            jax.ShapeDtypeStruct((1, 128), F32),
+            jax.ShapeDtypeStruct((2, 5, C, VW), F32),
+            jax.ShapeDtypeStruct((ns * np_, 128), F32),
         ),
         in_specs=[pl.BlockSpec(memory_space=pltpu.HBM)] * 10,
-        out_specs=(spec,) * 3,
+        out_specs=(pl.BlockSpec(memory_space=pltpu.HBM), spec),
         scratch_shapes=[
             vmem(2, 5, C, VW), vmem(2, 5, 3, C, FW), vmem(2, 5, 3, C, FW),
             vmem(2, 4, C, VW), vmem(3, 2, 4, C, FW), vmem(3, 2, 4, C, VW),
@@ -583,14 +612,30 @@
             vmem(2, tiles, 8, FW), vmem(2, tiles, 8, FW), vmem(2, C, 2 * FW), vmem(2, C, 2 * FW),
             vmem(1, 128), vmem(ns * np_, 1, 128),
             *[pltpu.VMEM(x.shape, x.dtype) for x in operands],
-            dma(8), dma(8), dma(ns * np_), dma(ns * np_), dma(10),
+            dma(8), dma(8), dma(ns * np_), dma(ns * np_), dma(10), dma(1),
         ],
         compiler_params=pltpu.CompilerParams(
             collective_id=0, has_side_effects=True, vmem_limit_bytes=63 * 1024 * 1024
         ),
         name="navier",
     )(*operands)
-    return residual, basis, krylov[0, :3]
+    hbm = pl.BlockSpec(memory_space=pltpu.HBM)
+    return pl.pallas_call(
+        functools.partial(finish, float(state.size * ns * np_)),
+        out_shape=(
+            jax.ShapeDtypeStruct(state.shape, F32),
+            jax.ShapeDtypeStruct(state.shape, F32),
+            jax.ShapeDtypeStruct((3,), F32),
+        ),
+        in_specs=[hbm] * 3,
+        out_specs=(hbm, hbm, spec),
+        scratch_shapes=[
+            vmem(2, 5, C, VW), vmem(C, L, width), vmem(ns * np_, 128),
+            vmem(C, L, width), vmem(C, L, width), dma(5),
+        ],
+        compiler_params=pltpu.CompilerParams(vmem_limit_bytes=63 * 1024 * 1024),
+        name="finish",
+    )(parts, direction, table)
 
 
 def solution(mesh):

time: 31 us -> 30.4 us (0.981)
  local copies, waits for them, and re-layouts: 3.54 us -> 0 us
  Pallas kernels: 26.7 us -> 29.6 us
    unnamed x6 -> x0, local copies, waits for them, and re-layouts: 3.03 us -> none
    pallas_call x1 -> x2, Pallas kernels: 26.7 us -> 29.6 us  [the longest x1 26 us: local(): pl.pallas_call(functools.partial(kernel, ns, np_), out_shape=(jax.ShapeDt...]
    squeeze x1 -> x0, local copies, waits for them, and re-layouts: 0.51 us -> none  [local(): return (residual, basis, krylov[0, :3])]
where the time goes in v4:
time: 30.4 us; the launch traced here: 30.2 us
  Pallas kernels  29.6 us (97%)
  between operations  0.64 us (2%)
    pallas_call x1, Pallas kernels, local(): pl.pallas_call(functools.partial(kernel, ns, np_), out_shape=(jax.ShapeDt...  26 us
    pallas_call x1, Pallas kernels, local(): pl.pallas_call(functools.partial(finish, float(state.size * ns * np_)), o...  3.62 us

profile of v4, /device:TPU:0, one launch (start us, length us, event | category | flops | bytes accessed | tf_op | source)
XLA Modules:
  0.0 30.2 jit_solution(7735654321472527623)
XLA Ops:
  0.6 26.0 %navier.1 = (f32[2,5,40,256]{3,2,1,0:T(8,128)}, f32[32,128]{1,0:T(8,128)}) custom-call(f32[40,2,625]{2,1,0:T(2,128)} %x_hbm.1, f32[40,2,625]{2,1,0:T(2,128)} %d_hbm.3, f32[3,2,40]{2,1,0:T(2,128)} %bitcast.2, s32[4,40]{1,0:T(4,128)} %bitcast.3, s32[1,2,33]{2,1,0:T(2,128)} %sr_hbm.1, s32[1,240]{1,0:T(1,128)} %constant.10.clone.key_hbm, ...), custom_call_target="tpu_custom_call" | custom-call | tf_op jit(solution)/shard_map/navier/pallas_call | solution.py:597
  26.6 3.6 %finish.1 = (f32[40,2,625]{2,1,0:T(2,128)}, f32[40,2,625]{2,1,0:T(2,128)}, f32[3]{0:T(128)}) custom-call(f32[2,5,40,256]{3,2,1,0:T(8,128)} %get-tuple-element.5.r_hbm, f32[40,2,625]{2,1,0:T(2,128)} %d_hbm.3, f32[32,128]{1,0:T(8,128)} %get-tuple-element.6.table_hbm), custom_call_target="tpu_custom_call" | custom-call | tf_op jit(solution)/shard_map/finish/pallas_call | solution.py:623

commit v5 on v4

--- a/solution.py
+++ b/solution.py
@@ -147,11 +147,11 @@
 def kernel(
     ns, np_,
     x_hbm, d_hbm, metric_hbm, fs_hbm, sr_hbm, key_hbm, dh_hbm, dl_hbm, pick_hbm, lift_hbm,
-    r_hbm, table_ref,
+    res_hbm, prod_hbm, table_ref,
     u, uf, of, w, jf, q, v, vf, ov, g, s, r, mv, mf,
     sb1, rb1, zs1, zr1, sb2, rb2, zs2, zr2, st, sta,
     x_ref, d_ref, metric_ref, fs_ref, sr_ref, keyrow_ref, dh_ref, dl_ref, pick_ref, lift_ref,
-    xsend, xrecv, asend, arecv, loads, store,
+    xsend, xrecv, asend, arecv, loads, store, res, prod,
 ):
     C, L = x_ref.shape[0], x_ref.shape[1]
     VW, FW, half = 128 * L, 64 * L, 32 * L
@@ -494,9 +494,6 @@
         lifted = part if lifted is None else lifted + part
     r[...] += lifted.reshape(2, 5, C, VW)
 
-    writing = pltpu.make_async_copy(r, r_hbm, store.at[0])
-    writing.start()
-
     def whole_sum(parts):
         acc = parts[0]
         for part in parts[1:]:
@@ -525,27 +522,34 @@
     for copy in copies:
         copy.start()
     sta[0] = st[...]
+    writes = []
+    for pt, (part, out) in enumerate([(res, res_hbm), (prod, prod_hbm)]):
+        for l in range(L):
+            for m in range(5):
+                part[:, l, 125 * m : 125 * (m + 1)] = r[pt, m, :, 128 * l : 128 * l + 125]
+        writes.append(pltpu.make_async_copy(part, out, store.at[pt]))
+        writes[pt].start()
     for copy in copies:
         copy.wait()
     table_ref[...] = sta[...].reshape(everyone, 128)
-    writing.wait()
+    for copy in writes:
+        copy.wait()
 
 
 def finish(
-    total_count, r_hbm, d_hbm, table_hbm, res_hbm, basis_hbm, kry_ref, r, d, table_ref, res, basis, sems
+    total_count, part_hbm, prod_hbm, d_hbm, table_hbm, res_hbm, basis_hbm, kry_ref,
+    res, prod, d, table_ref, basis, sems,
 ):
-    C, L = d.shape[0], d.shape[1]
     loads = [
         pltpu.make_async_copy(src, dst, sems.at[i])
-        for i, (src, dst) in enumerate([(r_hbm, r), (d_hbm, d), (table_hbm, table_ref)])
+        for i, (src, dst) in enumerate(
+            [(part_hbm, res), (table_hbm, table_ref), (d_hbm, d), (prod_hbm, prod)]
+        )
     ]
     for copy in loads:
         copy.start()
     loads[0].wait()
-    for l in range(L):
-        for m in range(5):
-            res[:, l, 125 * m : 125 * (m + 1)] = r[0, m, :, 128 * l : 128 * l + 125]
-    first = pltpu.make_async_copy(res, res_hbm, sems.at[3])
+    first = pltpu.make_async_copy(res, res_hbm, sems.at[4])
     first.start()
     for copy in loads[1:]:
         copy.wait()
@@ -563,12 +567,8 @@
     row = jnp.where(lane == 0, coefficient, jnp.where(lane == 1, beta, norm))
     kry_ref[...] = row[0, :3]
     c, inv = coefficient, 1.0 / beta
-    for l in range(L):
-        for m in range(5):
-            at = slice(125 * m, 125 * (m + 1))
-            product = r[1, m, :, 128 * l : 128 * l + 125]
-            basis[:, l, at] = (product - c * d[:, l, at]) * inv
-    second = pltpu.make_async_copy(basis, basis_hbm, sems.at[4])
+    basis[...] = (prod[...] - c[:, :, None] * d[...]) * inv[:, :, None]
+    second = pltpu.make_async_copy(basis, basis_hbm, sems.at[5])
     second.start()
     first.wait()
     second.wait()
@@ -594,14 +594,15 @@
     vmem = lambda *shape: pltpu.VMEM(shape, F32)
     dma = lambda n: pltpu.SemaphoreType.DMA((n,))
     spec = pl.BlockSpec(memory_space=pltpu.VMEM)
-    parts, table = pl.pallas_call(
+    parts, product, table = pl.pallas_call(
         functools.partial(kernel, ns, np_),
         out_shape=(
-            jax.ShapeDtypeStruct((2, 5, C, VW), F32),
+            jax.ShapeDtypeStruct(state.shape, F32),
+            jax.ShapeDtypeStruct(state.shape, F32),
             jax.ShapeDtypeStruct((ns * np_, 128), F32),
         ),
         in_specs=[pl.BlockSpec(memory_space=pltpu.HBM)] * 10,
-        out_specs=(pl.BlockSpec(memory_space=pltpu.HBM), spec),
+        out_specs=(pl.BlockSpec(memory_space=pltpu.HBM),) * 2 + (spec,),
         scratch_shapes=[
             vmem(2, 5, C, VW), vmem(2, 5, 3, C, FW), vmem(2, 5, 3, C, FW),
             vmem(2, 4, C, VW), vmem(3, 2, 4, C, FW), vmem(3, 2, 4, C, VW),
@@ -612,7 +613,7 @@
             vmem(2, tiles, 8, FW), vmem(2, tiles, 8, FW), vmem(2, C, 2 * FW), vmem(2, C, 2 * FW),
             vmem(1, 128), vmem(ns * np_, 1, 128),
             *[pltpu.VMEM(x.shape, x.dtype) for x in operands],
-            dma(8), dma(8), dma(ns * np_), dma(ns * np_), dma(10), dma(1),
+            dma(8), dma(8), dma(ns * np_), dma(ns * np_), dma(10), dma(2), vmem(C, L, width), vmem(C, L, width),
         ],
         compiler_params=pltpu.CompilerParams(
             collective_id=0, has_side_effects=True, vmem_limit_bytes=63 * 1024 * 1024
@@ -627,15 +628,15 @@
             jax.ShapeDtypeStruct(state.shape, F32),
             jax.ShapeDtypeStruct((3,), F32),
         ),
-        in_specs=[hbm] * 3,
+        in_specs=[hbm] * 4,
         out_specs=(hbm, hbm, spec),
         scratch_shapes=[
-            vmem(2, 5, C, VW), vmem(C, L, width), vmem(ns * np_, 128),
-            vmem(C, L, width), vmem(C, L, width), dma(5),
+            vmem(C, L, width), vmem(C, L, width), vmem(C, L, width), vmem(ns * np_, 128),
+            vmem(C, L, width), dma(6),
         ],
         compiler_params=pltpu.CompilerParams(vmem_limit_bytes=63 * 1024 * 1024),
         name="finish",
-    )(parts, direction, table)
+    )(parts, product, direction, table)
 
 
 def solution(mesh):

time: 30.4 us -> 29.8 us (0.980)
  Pallas kernels: 29.6 us -> 29 us
    pallas_call x1, Pallas kernels: 3.62 us -> 2.54 us  [local(): pl.pallas_call(functools.partial(finish, float(state.size * ns * np_)), o...]
    pallas_call x1, Pallas kernels: 26 us -> 26.5 us  [local(): pl.pallas_call(functools.partial(kernel, ns, np_), out_shape=(jax.ShapeDt...]
where the time goes in v5:
time: 29.8 us; the launch traced here: 29.6 us
  Pallas kernels  29 us (97%)
  between operations  0.64 us (2%)
    pallas_call x1, Pallas kernels, local(): pl.pallas_call(functools.partial(kernel, ns, np_), out_shape=(jax.ShapeDt...  26.5 us
    pallas_call x1, Pallas kernels, local(): pl.pallas_call(functools.partial(finish, float(state.size * ns * np_)), o...  2.54 us

profile of v5, /device:TPU:0, one launch (start us, length us, event | category | flops | bytes accessed | tf_op | source)
XLA Modules:
  0.0 29.6 jit_solution(8627987812115112573)
XLA Ops:
  0.6 26.5 %navier.1 = (f32[40,2,625]{2,1,0:T(2,128)}, f32[40,2,625]{2,1,0:T(2,128)}, f32[32,128]{1,0:T(8,128)}) custom-call(f32[40,2,625]{2,1,0:T(2,128)} %x_hbm.1, f32[40,2,625]{2,1,0:T(2,128)} %d_hbm.3, f32[3,2,40]{2,1,0:T(2,128)} %bitcast.2, s32[4,40]{1,0:T(4,128)} %bitcast.3, s32[1,2,33]{2,1,0:T(2,128)} %sr_hbm.1, s32[1,240]{1,0:T(1,128)} %constant.10.clone.key_hbm, ...), custom_call_target="tpu_custom_call" | custom-call | tf_op jit(solution)/shard_map/navier/pallas_call | solution.py:597
  27.1 2.5 %finish.1 = (f32[40,2,625]{2,1,0:T(2,128)}, f32[40,2,625]{2,1,0:T(2,128)}, f32[3]{0:T(128)}) custom-call(f32[40,2,625]{2,1,0:T(2,128)} %get-tuple-element.6.part_hbm, f32[40,2,625]{2,1,0:T(2,128)} %get-tuple-element.7.prod_hbm, f32[40,2,625]{2,1,0:T(2,128)} %d_hbm.3, f32[32,128]{1,0:T(8,128)} %get-tuple-element.8.table_hbm), custom_call_target="tpu_custom_call" | custom-call | tf_op jit(solution)/shard_map/finish/pallas_call | solution.py:624
